TPU v7x, 32 devices: a whole 2x2x4 slice. The times are simulated.
32 devices in a mesh: sweep: 2 (over x), expert: 4 (over y, core), fsdp: 4 (over z).
Axes of the slice: x: 2, y: 2, z: 4, core: 2. Of those that a mesh axis runs over, the one named last changes fastest.
Arguments:
- tokens: bfloat16 [4096, 2048], P(('sweep', 'expert', 'fsdp')), parts along dimension 0, may hold values from -6 to 6
- context: bfloat16 [4096, 2048], P(('sweep', 'expert', 'fsdp')), parts along dimension 0, may hold values from -6 to 6
- out_proj: bfloat16 [4096, 2048], P(('sweep', 'expert', 'fsdp')), parts along dimension 0, may hold values from -0.125 to 0.125
- norm_gain: float32 [4096], P('sweep'), parts along dimension 0, may hold values from 0.1 to 1.9
- router: bfloat16 [4096, 8], P('sweep'), parts along dimension 0, may hold values from -0.125 to 0.125
- expert_ids: int32 [4096, 2], P(('sweep', 'expert', 'fsdp')), parts along dimension 0, may hold values from 0 to 7, all different within a row; in each aligned block of 128 rows (0 to 127, 128 to 255, ...) at most 40 rows name the same one
- w_gate_up: bfloat16 [32, 2, 704, 2048], P(('sweep', 'expert', 'fsdp')), parts along dimension 0, may hold values from -0.125 to 0.125
- w_down: bfloat16 [32, 704, 2048], P(('sweep', 'expert', 'fsdp')), parts along dimension 0, may hold values from -0.15625 to 0.15625
Outputs:
- layer_out: bfloat16 [4096, 2048], P(('sweep', 'expert', 'fsdp')), parts along dimension 0
There are 2 independent parts, one for each index of `sweep`. A program takes and returns all parts, laid end to end along the dimension named above; each array names one. Nothing has to cross between parts.
Inputs may be any that keep to these rules, and one draw needn't show every extreme that they name: `expert_ids`: each row names two different experts. Among the rows of one device no expert is named more than 40 times, a bound that some block reaches.
All inputs are finite; a program needn't handle non-finite values.
Results may differ from a plain program's by a relative error of at most 0.012.
Values may be sent and summed in bfloat16 or wider, within the bound.
A program may use at most 64 MiB of HBM per device.

v0:
```python
import jax
import jax.numpy as jnp
from jax import lax
from jax.sharding import PartitionSpec as P

eps_norm = 1e-05


def half_block(taken, gate_up_w, down_w):
    gate_up = jnp.einsum("rd,kfd->krf", taken, gate_up_w, preferred_element_type=jnp.float32)
    hidden = (jax.nn.silu(gate_up[0]) * gate_up[1]).astype(jnp.bfloat16)
    return jnp.dot(hidden, down_w, preferred_element_type=jnp.float32).astype(jnp.bfloat16)


def slot_places(expert_ids, experts):
    flat_ids = expert_ids.reshape(-1)
    onehot = (flat_ids[:, None] == jnp.arange(experts, dtype=jnp.int32)[None, :]).astype(jnp.int32)
    before = jnp.cumsum(onehot, axis=0) - onehot
    places = jnp.sum(before * onehot, axis=1)
    return (flat_ids, places)


def on_device(tokens, context, out_proj, norm_gain, router, expert_ids, w_gate_up, w_down):
    rows_here, width = tokens.shape
    columns = lax.axis_size("expert")
    members = lax.axis_size("fsdp")
    experts = columns * members // 2
    slot_cap = 5 * rows_here // (2 * experts)
    gate_up_here = w_gate_up[0]
    down_here = w_down[0]
    attended = jnp.dot(
        context,
        lax.all_gather(out_proj, ("expert", "fsdp"), axis=0, tiled=True),
        preferred_element_type=jnp.float32,
    )
    residual_in = (tokens.astype(jnp.float32) + attended).astype(jnp.bfloat16)
    widened = residual_in.astype(jnp.float32)
    inv_rms = lax.rsqrt(jnp.mean(widened * widened, axis=1, keepdims=True) + eps_norm)
    normed = (widened * inv_rms * norm_gain).astype(jnp.bfloat16)
    logits = jnp.dot(normed, router, preferred_element_type=jnp.float32)
    picked = jnp.take_along_axis(logits, expert_ids, axis=1)
    scores = jax.nn.sigmoid(picked)
    gate_vals = scores / jnp.sum(scores, axis=1, keepdims=True)
    flat_ids, places = slot_places(expert_ids, experts)
    source_rows = jnp.repeat(normed, 2, axis=0)
    empty_box = jnp.zeros((experts * slot_cap, width), jnp.bfloat16)
    target = flat_ids * slot_cap + places
    outbox = empty_box.at[target].set(source_rows).reshape(experts, slot_cap, width)
    copies = jnp.broadcast_to(outbox[:, None], (experts, 2, slot_cap, width))
    copies = copies.reshape(2 * experts, slot_cap, width)
    pieces = lax.all_to_all(copies, ("expert", "fsdp"), split_axis=0, concat_axis=0, tiled=True)
    senders = pieces.shape[0]
    slots_in = pieces.shape[1]
    output_half = half_block(pieces.reshape(senders * slots_in, width), gate_up_here, down_here)
    partials = output_half.reshape(senders, slots_in, width)
    returned = lax.all_to_all(partials, ("expert", "fsdp"), split_axis=0, concat_axis=0, tiled=True)
    halves = returned.reshape(experts, 2, slot_cap, width).astype(jnp.float32)
    finished = (halves[:, 0] + halves[:, 1]).astype(jnp.bfloat16)
    results = finished.reshape(-1, width)[target].astype(jnp.float32).reshape(rows_here, 2, width)
    output_rows = widened + gate_vals[:, 0:1] * results[:, 0] + gate_vals[:, 1:2] * results[:, 1]
    return output_rows.astype(jnp.bfloat16)


def solution(mesh):
    return jax.shard_map(
        on_device,
        mesh=mesh,
        in_specs=(
            P(("sweep", "expert", "fsdp"), None),
            P(("sweep", "expert", "fsdp"), None),
            P(("sweep", "expert", "fsdp"), None),
            P("sweep"),
            P("sweep", None),
            P(("sweep", "expert", "fsdp"), None),
            P(("sweep", "expert", "fsdp"), None, None, None),
            P(("sweep", "expert", "fsdp"), None, None),
        ),
        out_specs=P(("sweep", "expert", "fsdp"), None),
        check_vma=False,
    )
```

profile of v0, /device:TPU:0, one launch (start us, length us, event | category | flops | bytes accessed | tf_op | source)
XLA Modules:
  0.0 267.1 jit_solution(5074877685539028530)
XLA Ops:
  6.5 0.7 all-gather.2.cloned.1.call-update
  7.3 0.9 copy.38
  8.5 0.7 broadcast_multiply_fusion
  9.4 0.6 reduce-window.6
  10.4 76.2 %all-gather.2.cloned.1.call-done = bf16[2048,2048]{1,0:T(8,128)(2,1)} async-done(((bf16[128,2048]{1,0:T(8,128)(2,1)}), bf16[2048,2048]{1,0:T(8,128)(2,1)}) %all-gather.2.cloned.1.call-update) | async-done | bytes 8388624 | tf_op jit(solution)/shard_map/all_gather | solution.py:33
  86.6 5.0 %multiply_reduce_fusion = (f32[128]{0:T(128)S(1)}, f32[128,2048]{1,0:T(8,128)S(1)}) fusion(bf16[128,2048]{1,0:T(8,128)(2,1)} %param.9, bf16[2048,2048]{1,0:T(8,128)(2,1)} %all-gather.2.cloned.1.call-done, bf16[128,2048]{1,0:T(8,128)(2,1)} %param.8), kind=kOutput, calls=%fused_computation.25 | convolution fusion | flops 1075314560 | bytes 10486272 | tf_op jit(solution)/shard_map/dot_general | solution.py:31
  91.6 1.0 copy-done.1
  92.8 1.6 broadcast_in_dim.25
  94.4 2.3 reshape.117
  96.6 4.0 %scatter_custom_fusion = bf16[320,2048]{1,0:T(8,128)(2,1)} fusion(s32[256]{0:T(256)S(1)} %bitcast.77, bf16[256,2048]{1,0:T(8,128)(2,1)} %reshape.117, bf16[]{:T(256)} %constant.36.clone.1), kind=kCustom, calls=%fused_computation.27 | custom fusion | bytes 1311232 | tf_op jit(solution)/shard_map/scatter | solution.py:48
  100.6 1.7 broadcast_in_dim.27
  102.3 63.7 %all_to_all.10 = bf16[16,40,2048]{2,1,0:T(8,128)(2,1)S(1)} all-to-all(bf16[16,40,2048]{2,1,0:T(8,128)(2,1)S(1)} %bitcast.73), channel_id=1, replica_groups=mesh['sweep'=2,'expert'=4,'fsdp'=4] {'expert','fsdp'}, dimensions={0} | all-to-all | bytes 5242880 | tf_op jit(solution)/shard_map/all_to_all | solution.py:51
  166.0 6.7 %fusion.7 = f32[2,640,704]{1,2,0:T(8,128)S(1)} fusion(bf16[640,2048,1]{1,0,2:T(8,128)(2,1)S(1)} %bitcast.76, bf16[1,2,704,2048]{3,2,1,0:T(8,128)(2,1)} %param.14), kind=kOutput, calls=%fused_computation.14 | convolution fusion | flops 3690987520 | bytes 11993088 | tf_op jit(solution)/shard_map/rd,kfd->krf/dot_general | solution.py:10
  172.7 3.9 %convolution_convert_fusion = bf16[640,2048]{1,0:T(8,128)(2,1)} fusion(bf16[1,704,2048]{2,1,0:T(8,128)(2,1)S(1)} %copy-done, f32[2,640,704]{1,2,0:T(8,128)S(1)} %fusion.7), kind=kOutput, calls=%fused_computation.5 | convolution fusion | flops 1849507840 | bytes 9109504 | tf_op jit(solution)/shard_map/dot_general | solution.py:12
  176.6 4.8 %all-to-all-start.1 = ((bf16[16,40,2048]{2,1,0:T(8,128)(2,1)}), bf16[16,40,2048]{2,1,0:T(8,128)(2,1)}, u32[]{:S(2)}, u32[]{:S(2)}) async-start(bf16[16,40,2048]{2,1,0:T(8,128)(2,1)} %bitcast.75), calls=%async_computation.1 | async-start | bytes 5242880 | tf_op jit(solution)/shard_map/all_to_all | solution.py:56
  181.7 0.2 fusion.26
  181.9 1.4 gather_fusion.1
  183.6 58.2 %all-to-all-done.1 = bf16[16,40,2048]{2,1,0:T(8,128)(2,1)} async-done(((bf16[16,40,2048]{2,1,0:T(8,128)(2,1)}), bf16[16,40,2048]{2,1,0:T(8,128)(2,1)}, u32[]{:S(2)}, u32[]{:S(2)}) %all-to-all-start.1) | async-done | bytes 2621472 | tf_op jit(solution)/shard_map/all_to_all | solution.py:56
  241.8 2.4 convert.2
  244.2 1.4 fusion.4
  245.6 4.8 %gather_fusion = bf16[256,2048]{1,0:T(8,128)(2,1)} fusion(bf16[320,2048]{1,0:T(8,128)(2,1)} %bitcast.72, s32[1024]{0:T(1024)S(1)} %pad_clamp_fusion), kind=kCustom, calls=%fused_computation | custom fusion | bytes 2098176 | tf_op jit(solution)/shard_map/gather | solution.py:59
  250.5 3.4 %reshape.98 = f32[128,2,2048]{2,1,0:T(2,128)} reshape(bf16[256,2048]{1,0:T(8,128)(2,1)} %gather_fusion) | data formatting | bytes 3145728 | tf_op jit(solution)/shard_map/convert_element_type | solution.py:59
  253.8 4.5 %fusion.25 = (f32[128,1,2048]{2,1,0:T(1,128)S(1)}, f32[128,1,2048]{2,1,0:T(1,128)S(1)}) fusion(f32[128,2,2048]{2,1,0:T(2,128)} %reshape.98), kind=kLoop, calls=%fused_computation.50 | loop fusion | bytes 4194304 | tf_op jit(solution)/shard_map/slice | solution.py:60
  258.3 1.9 fusion.13
  (33 shorter events, 1.6 us)
Async XLA Ops:
  6.5 166.2 %copy-start = (bf16[1,704,2048]{2,1,0:T(8,128)(2,1)S(1)}, bf16[1,704,2048]{2,1,0:T(8,128)(2,1)}, u32[]{:S(2)}) copy-start(bf16[1,704,2048]{2,1,0:T(8,128)(2,1)} %param.15) | copy-start | bytes 8650756
  6.5 80.1 %all-gather.2.cloned.1.call-start = ((), (), s32[]{:S(2)}) async-start(), calls=%async_computation.2 | async-start | bytes 8912896 | tf_op jit(solution)/shard_map/all_gather | solution.py:33
  10.4 82.2 %copy-start.5 = (f32[2048]{0:T(1024)S(1)}, f32[2048]{0:T(1024)}, u32[]{:S(2)}) copy-start(f32[2048]{0:T(1024)} %param.11) | copy-start | bytes 24580
  91.6 1.0 copy-start.1
  176.6 4.8 %copy-start.4 = (s32[128,2]{0,1:T(2,128)S(1)}, s32[128,2]{0,1:T(2,128)}, u32[]{:S(2)}) copy-start(s32[128,2]{0,1:T(2,128)} %param.13) | copy-start | bytes 3076
  176.6 5.1 %copy-start.3 = (bf16[2048,8]{0,1:T(8,128)(2,1)S(1)}, bf16[2048,8]{0,1:T(8,128)(2,1)}, u32[]{:S(2)}) copy-start(bf16[2048,8]{0,1:T(8,128)(2,1)} %param.12) | copy-start | bytes 98308
  176.6 65.2 %all-to-all-start.1 = ((bf16[16,40,2048]{2,1,0:T(8,128)(2,1)}), bf16[16,40,2048]{2,1,0:T(8,128)(2,1)}, u32[]{:S(2)}, u32[]{:S(2)}) async-start(bf16[16,40,2048]{2,1,0:T(8,128)(2,1)} %bitcast.75), calls=%async_computation.1 | async-start | bytes 5242880 | tf_op jit(solution)/shard_map/all_to_all | solution.py:56
  253.8 4.5 %copy-start.2 = (f32[128,2048]{1,0:T(8,128)S(1)}, f32[128,2048]{1,0:T(8,128)}, u32[]{:S(2)}) copy-start(f32[128,2048]{1,0:T(8,128)} %copy-done.1) | copy-start | bytes 3145732
Sparse Core Ops, SparseCore 0:
  9.5 77.0 all-gather.1
where the time goes:
time: 268 us; the launch traced here: 267 us
  waiting for transfers between devices  135 us (50%)
  blocking collectives  63.7 us (24%)
  local copies, waits for them, and re-layouts  26.7 us (10%)
  matrix products  15.8 us (6%)
  between operations  13.6 us (5%)
  other arithmetic  7.37 us (3%)
  starting transfers between devices  4.76 us (2%)
    all_gather x1, waiting for transfers between devices, on_device(): lax.all_gather(out_proj, ('expert', 'fsdp'), axis=0, tiled=True)  76.2 us
    all_to_all x1, blocking collectives, on_device(): lax.all_to_all(copies, ('expert', 'fsdp'), split_axis=0, concat_axis=0, t...  63.7 us
    all_to_all x1, waiting for transfers between devices, on_device(): lax.all_to_all(partials, ('expert', 'fsdp'), split_axis=0, concat_axis=0,...  58.2 us
    dot_general x1, matrix products, half_block(): jnp.einsum('rd,kfd->krf', taken, gate_up_w, preferred_element_type=jnp.fl...  6.72 us
  transfers between devices with their start and end apart: 2, of which 2 were waited for; matrix products, arithmetic and copies ran while one was open for 2% of the time, Pallas kernels for 0%

commit v1 on v0

v1 whole, which is shorter than its diff:
```python
import functools

import jax
import jax.numpy as jnp
from jax import lax
from jax.experimental import pallas as pl
from jax.experimental.pallas import tpu as pltpu
from jax.sharding import PartitionSpec as P

eps_norm = 1e-05
MESH = pl.DeviceIdType.MESH
VMEM_GRANT = 60 * 1024 * 1024


def both(a, b):
    return jnp.logical_and(a, b)


def inside(i, n):
    return both(i >= 0, i < n)


def block_kernel(
    columns, members, cap, slots,
    tok, ctx, wout, gain, router, ids, gu_hbm, dn_hbm,
    out,
    gath, acc, gu, dn, outbox, inbox, part, partner, ret, resid,
    load_sem, ag_send, ag_recv, disp_send, disp_recv, fwd_send,
    part_send, part_recv, ret_send, ret_recv,
):
    n = columns * members
    lines = columns // 2
    pairs = members // 2
    experts = columns * pairs
    rows, width = tok.shape
    k_rows = wout.shape[0]
    my_e = lax.axis_index("expert")
    my_f = lax.axis_index("fsdp")
    me = my_e * members + my_f
    my_y, my_c = lax.div(my_e, 2), lax.rem(my_e, 2)
    my_p = lax.div(my_f, 2)
    my_expert = my_e * pairs + my_p

    def dev(e, f):
        return {"expert": e, "fsdp": f}

    load_gu = pltpu.make_async_copy(gu_hbm.at[0], gu, load_sem.at[0])
    load_dn = pltpu.make_async_copy(dn_hbm.at[0], dn, load_sem.at[1])
    load_gu.start()
    load_dn.start()

    barrier = pltpu.get_barrier_semaphore()

    def greet(i, _):
        other = lax.rem(me + i, n)
        pl.semaphore_signal(
            barrier, inc=1, device_id=dev(lax.div(other, members), lax.rem(other, members)),
            device_id_type=MESH)
        return 0

    lax.fori_loop(1, n, greet, 0)
    pl.semaphore_wait(barrier, n - 1)

    def place(e, f):
        return pl.ds(pl.multiple_of((e * members + f) * k_rows, k_rows), k_rows)

    def ag(e, f, way, target, own=False):
        b = e * members + f
        return pltpu.make_async_remote_copy(
            src_ref=wout if own else gath.at[place(e, f)],
            dst_ref=gath.at[place(e, f)],
            send_sem=ag_send.at[b, way],
            recv_sem=ag_recv.at[b],
            device_id=target,
            device_id_type=MESH)

    def ag_arrived(e, f):
        ag(e, f, 0, dev(my_y * 2 + 1 - my_c, my_f)).wait_recv()

    def z_copies(s, sign):
        fb, to = my_f + sign * s, my_f - sign
        k = 0 if sign == 1 else 1
        own = s == 0
        result = [(inside(to, members), lambda: ag(my_e, fb, k, dev(my_e, jnp.clip(to, 0, members - 1)), own))]
        if s > 0 or sign == 1:
            for j, ysign in enumerate((1, -1)):
                yt = my_y - ysign
                result.append((
                    inside(yt, lines),
                    lambda yt=yt, j=j: ag(my_e, fb, 2 + j, dev(jnp.clip(yt, 0, lines - 1) * 2 + my_c, my_f), own)))
            result.append((None, lambda: ag(my_e, fb, 4, dev(my_y * 2 + 1 - my_c, my_f), own)))
        return inside(fb, members), fb, result

    def y_copies(t, s, sign, ysign):
        fb = my_f + sign * s
        yb, yt = my_y + ysign * t, my_y - ysign
        e_b = yb * 2 + my_c
        j = 0 if ysign == 1 else 1
        result = []
        if t < lines - 1:
            result.append((
                inside(yt, lines),
                lambda: ag(e_b, fb, 2 + j, dev(jnp.clip(yt, 0, lines - 1) * 2 + my_c, my_f))))
        result.append((None, lambda: ag(e_b, fb, 4, dev(my_y * 2 + 1 - my_c, my_f))))
        return both(inside(fb, members), inside(yb, lines)), e_b, fb, result

    def apply(result, finish):
        for cond, make in result:
            def go(make=make):
                if finish:
                    make().wait_send()
                else:
                    make().start()
            if cond is None:
                go()
            else:
                pl.when(cond)(go)

    def z_step(s, finish=False):
        for sign in (1, -1):
            ok, fb, result = z_copies(s, sign)

            @pl.when(ok)
            def _():
                if s > 0 and not finish:
                    ag_arrived(my_e, fb)
                apply(result, finish)

    def y_step(t, s, finish=False):
        for ysign in (1, -1):
            for sign in (1, -1) if s else (1,):
                ok, e_b, fb, result = y_copies(t, s, sign, ysign)

                @pl.when(ok)
                def _():
                    if not finish:
                        ag_arrived(e_b, fb)
                    apply(result, finish)

    depth = members * k_rows
    col = min(512, width)

    def multiply(e):
        at = pl.ds(pl.multiple_of(e * depth, depth), depth)
        a = ctx[:, at]

        def one(i, _):
            cols = pl.ds(pl.multiple_of(i * col, col), col)
            acc[:, cols] += jnp.dot(a, gath[at, cols], preferred_element_type=jnp.float32)
            return 0

        lax.fori_loop(0, width // col, one, 0)

    z_step(0)
    gath[place(my_e, my_f), :] = wout[...]
    acc[...] = tok[...].astype(jnp.float32)
    for s in range(1, members):
        z_step(s)
        if lines > 1:
            y_step(1, s - 1)
    multiply(my_e)
    if lines > 1:
        y_step(1, members - 1)
        for t in range(2, lines):
            for s in range(members):
                y_step(t, s)

    id0, id1 = ids[:, 0:1], ids[:, 1:2]
    named = lax.broadcasted_iota(jnp.int32, (rows, experts), 1)
    hot0 = jnp.where(named == id0, 1.0, 0.0)
    hot1 = jnp.where(named == id1, 1.0, 0.0)
    earlier = jnp.where(
        lax.broadcasted_iota(jnp.int32, (rows, rows), 1) < lax.broadcasted_iota(jnp.int32, (rows, rows), 0),
        1.0, 0.0).astype(jnp.bfloat16)
    before = jnp.dot(earlier, (hot0 + hot1).astype(jnp.bfloat16), preferred_element_type=jnp.float32)
    slot0 = id0 * slots + jnp.sum(before * hot0, axis=1, keepdims=True).astype(jnp.int32)
    slot1 = id1 * slots + jnp.sum(before * hot1, axis=1, keepdims=True).astype(jnp.int32)
    slot_no = lax.broadcasted_iota(jnp.int32, (rows, experts * slots), 1)
    at0, at1 = slot_no == slot0, slot_no == slot1
    send_mask = jnp.where(jnp.logical_or(at0, at1), 1.0, 0.0).astype(jnp.bfloat16)

    def other_lines(t, _):
        multiply(lax.rem(my_y + t, lines) * 2 + my_c)
        return 0

    lax.fori_loop(1, lines, other_lines, 0)

    def other_core(t, _):
        e = lax.rem(my_y + t, lines) * 2 + 1 - my_c

        def one(f, _):
            ag_arrived(e, f)
            return 0

        lax.fori_loop(0, members, one, 0)
        multiply(e)
        return 0

    lax.fori_loop(0, lines, other_core, 0)

    rounded = acc[...].astype(jnp.bfloat16)
    resid[...] = rounded
    widened = rounded.astype(jnp.float32)
    inv = lax.rsqrt(jnp.mean(widened * widened, axis=1, keepdims=True) + eps_norm)
    normed = (widened * inv * gain[...]).astype(jnp.bfloat16)
    boxes = lax.dot_general(
        send_mask, normed, (((0,), (0,)), ((), ())), preferred_element_type=jnp.float32
    ).astype(jnp.bfloat16)
    for e in range(experts):
        outbox[e] = boxes[e * slots:(e + 1) * slots]

    def near_of(f, p):
        return jnp.clip(f, 2 * p, 2 * p + 1)

    def dispatch(e, p):
        x = e * pairs + p
        return pltpu.make_async_remote_copy(
            src_ref=outbox.at[x], dst_ref=inbox.at[me],
            send_sem=disp_send.at[x], recv_sem=disp_recv.at[me],
            device_id=dev(e, near_of(my_f, p)), device_id_type=MESH)

    def each_target(finish):
        for q in range(1, pairs + 1):
            p = lax.rem(my_p + q, pairs)

            def one(i, _):
                e = lax.rem(my_e + i, columns)
                if finish:
                    dispatch(e, p).wait_send()
                else:
                    dispatch(e, p).start()
                return 0

            lax.fori_loop(0 if q < pairs else 1, columns, one, 0)

    each_target(False)
    inbox[me] = outbox[my_expert]

    far_f = 4 * my_p + 1 - my_f

    def forward(b):
        return pltpu.make_async_remote_copy(
            src_ref=inbox.at[b], dst_ref=inbox.at[b],
            send_sem=fwd_send.at[b], recv_sem=disp_recv.at[b],
            device_id=dev(my_e, far_f), device_id_type=MESH)

    def group_of(g):
        return lax.rem(2 * my_p + g, members)

    def i_am_near(fs):
        return near_of(fs, my_p) == my_f

    def box_of(fs, i):
        return lax.rem(my_e + i, columns) * members + fs

    def pass_on(g):
        fs = group_of(g)

        def one(i, _):
            b = box_of(fs, i)

            @pl.when(b != me)
            def _():
                forward(b).wait_recv()

            @pl.when(i_am_near(fs))
            def _():
                forward(b).start()
            return 0

        lax.fori_loop(0, columns, one, 0)

    def give(b):
        return pltpu.make_async_remote_copy(
            src_ref=part.at[b], dst_ref=partner.at[b],
            send_sem=part_send.at[b], recv_sem=part_recv.at[b],
            device_id=dev(my_e, far_f), device_id_type=MESH)

    def give_back(b):
        return pltpu.make_async_remote_copy(
            src_ref=part.at[b], dst_ref=ret.at[my_expert],
            send_sem=ret_send.at[b], recv_sem=ret_recv.at[my_expert],
            device_id=dev(lax.div(b, members), lax.rem(b, members)), device_id_type=MESH)

    nt = (((1,), (1,)), ((), ()))

    def expert(g):
        fs = group_of(g)
        x = jnp.concatenate([inbox[e * members + fs] for e in range(columns)], axis=0)
        gate = lax.dot_general(x, gu[0], nt, preferred_element_type=jnp.float32)
        up = lax.dot_general(x, gu[1], nt, preferred_element_type=jnp.float32)
        hidden = (gate / (1.0 + jnp.exp(-gate)) * up).astype(jnp.bfloat16)
        piece = jnp.dot(hidden, dn[...], preferred_element_type=jnp.float32).astype(jnp.bfloat16)
        for e in range(columns):
            part[e * members + fs] = piece[e * slots:(e + 1) * slots]

        @pl.when(jnp.logical_not(i_am_near(fs)))
        def _():
            def one(i, _):
                give(box_of(fs, i)).start()
                return 0

            lax.fori_loop(0, columns, one, 0)

    def finish_group(g):
        fs = group_of(g)

        @pl.when(i_am_near(fs))
        def _():
            def one(i, _):
                b = box_of(fs, i)
                give(b).wait_recv()
                part[b] = (part[b].astype(jnp.float32) + partner[b].astype(jnp.float32)).astype(jnp.bfloat16)

                @pl.when(b == me)
                def _():
                    ret[my_expert] = part[b]

                @pl.when(b != me)
                def _():
                    give_back(b).start()
                return 0

            lax.fori_loop(0, columns, one, 0)

    logits = jnp.dot(normed, router[...], preferred_element_type=jnp.float32)
    s0 = jax.nn.sigmoid(jnp.sum(logits * hot0, axis=1, keepdims=True))
    s1 = jax.nn.sigmoid(jnp.sum(logits * hot1, axis=1, keepdims=True))
    total = s0 + s1
    weights = jnp.where(at0, s0 / total, 0.0) + jnp.where(at1, s1 / total, 0.0)
    weights_high = weights.astype(jnp.bfloat16)
    weights_low = (weights - weights_high.astype(jnp.float32)).astype(jnp.bfloat16)

    load_gu.wait()
    load_dn.wait()

    pass_on(0)

    def step(g, _):
        @pl.when(g + 1 < members)
        def _():
            pass_on(g + 1)

        expert(g)

        @pl.when(g > 0)
        def _():
            finish_group(g - 1)
        return 0

    lax.fori_loop(0, members, step, 0)
    finish_group(members - 1)

    def came_back(x, _):
        @pl.when(x != my_expert)
        def _():
            pltpu.make_async_remote_copy(
                src_ref=ret.at[x], dst_ref=ret.at[x],
                send_sem=disp_send.at[x], recv_sem=ret_recv.at[x],
                device_id=dev(my_e, far_f), device_id_type=MESH).wait_recv()
        return 0

    lax.fori_loop(0, experts, came_back, 0)
    results = jnp.concatenate([ret[x] for x in range(experts)], axis=0)
    mixed = jnp.dot(weights_high, results, preferred_element_type=jnp.float32)
    mixed = mixed + jnp.dot(weights_low, results, preferred_element_type=jnp.float32)
    out[...] = (resid[...].astype(jnp.float32) + mixed).astype(jnp.bfloat16)

    for s in range(members):
        z_step(s, True)
        for t in range(1, lines):
            y_step(t, s, True)
    each_target(True)

    def drain(b, _):
        fs = lax.rem(b, members)
        mine = lax.div(b, members)

        @pl.when(i_am_near(fs))
        def _():
            forward(b).wait_send()

            @pl.when(b != me)
            def _():
                give_back(b).wait_send()

        @pl.when(jnp.logical_not(i_am_near(fs)))
        def _():
            give(b).wait_send()
        return 0

    lax.fori_loop(0, n, drain, 0)


def on_device(tokens, context, out_proj, norm_gain, router, expert_ids, w_gate_up, w_down):
    rows, width = tokens.shape
    columns = lax.axis_size("expert")
    members = lax.axis_size("fsdp")
    n = columns * members
    experts = n // 2
    cap = 5 * rows // (2 * experts)
    slots = -(-cap // 8) * 8
    units = w_down.shape[1]
    vmem = pl.BlockSpec(memory_space=pltpu.VMEM)
    far = pl.BlockSpec(memory_space=pl.ANY)
    bf = jnp.bfloat16
    dma = pltpu.SemaphoreType.DMA
    call = pl.pallas_call(
        functools.partial(block_kernel, columns, members, cap, slots),
        out_shape=jax.ShapeDtypeStruct((rows, width), bf),
        in_specs=[vmem] * 6 + [far] * 2,
        out_specs=vmem,
        scratch_shapes=[
            pltpu.VMEM((n * out_proj.shape[0], width), bf),
            pltpu.VMEM((rows, width), jnp.float32),
            pltpu.VMEM((2, units, width), bf),
            pltpu.VMEM((units, width), bf),
            pltpu.VMEM((experts, slots, width), bf),
            pltpu.VMEM((n, slots, width), bf),
            pltpu.VMEM((n, slots, width), bf),
            pltpu.VMEM((n, slots, width), bf),
            pltpu.VMEM((experts, slots, width), bf),
            pltpu.VMEM((rows, width), bf),
            dma((2,)), dma((n, 5)), dma((n,)), dma((experts,)), dma((n,)), dma((n,)),
            dma((n,)), dma((n,)), dma((n,)), dma((experts,)),
        ],
        compiler_params=pltpu.CompilerParams(
            collective_id=0, has_side_effects=True, vmem_limit_bytes=VMEM_GRANT),
    )
    return call(tokens, context, out_proj, norm_gain.reshape(1, width), router, expert_ids, w_gate_up, w_down)


def solution(mesh):
    group = ("sweep", "expert", "fsdp")
    return jax.shard_map(
        on_device,
        mesh=mesh,
        in_specs=(
            P(group, None), P(group, None), P(group, None), P("sweep"), P("sweep", None),
            P(group, None), P(group, None, None, None), P(group, None, None),
        ),
        out_specs=P(group, None),
        check_vma=False,
    )
```

time: 268 us -> 203 us (0.76)
  the two profiles are of different devices: /device:TPU:0 before, /device:TPU:25 now
where the time goes in v1:
time: 203 us
  Pallas kernels  198 us (98%)
  local copies, waits for them, and re-layouts  5.05 us (2%)
    pallas_call x1, Pallas kernels, on_device(): call(tokens, context, out_proj, norm_gain.reshape(1, width), router, expe...  198 us
    unnamed x3, local copies, waits for them, and re-layouts  5.05 us

profile of v1, /device:TPU:25, one launch (start us, length us, event | category | flops | bytes accessed | tf_op | source)
XLA Modules:
  0.0 202.7 jit_solution(15584721277220791593)
XLA Ops:
  0.0 1.4 copy.10.ids
  1.4 1.8 copy.9.router
  3.2 197.6 %shard_map.82 = bf16[128,2048]{1,0:T(8,128)(2,1)} custom-call(bf16[128,2048]{1,0:T(8,128)(2,1)} %tok.1, bf16[128,2048]{1,0:T(8,128)(2,1)} %ctx.1, bf16[128,2048]{1,0:T(8,128)(2,1)} %wout.1, f32[1,2048]{1,0:T(1,128)} %bitcast.1, bf16[2048,8]{1,0:T(8,128)(2,1)} %copy.9.router, s32[128,2]{1,0:T(8,128)} %copy.10.ids, bf16[1,2,704,2048]{3,2,1,0:T(8,128)(2,1)} %gu_hbm.1, ...), custom_call_target="tpu_custom_call" | custom-call | tf_op jit(solution)/shard_map/pallas_call | solution.py:430
  200.8 1.9 copy.12

commit v2 on v1

--- a/solution.py
+++ b/solution.py
@@ -220,7 +220,7 @@
             device_id=dev(e, near_of(my_f, p)), device_id_type=MESH)
 
     def each_target(finish):
-        for q in range(1, pairs + 1):
+        for q in range(pairs):
             p = lax.rem(my_p + q, pairs)
 
             def one(i, _):
@@ -231,7 +231,7 @@
                     dispatch(e, p).start()
                 return 0
 
-            lax.fori_loop(0 if q < pairs else 1, columns, one, 0)
+            lax.fori_loop(0 if q else 1, columns, one, 0)
 
     each_target(False)
     inbox[me] = outbox[my_expert]
@@ -244,8 +244,11 @@
             send_sem=fwd_send.at[b], recv_sem=disp_recv.at[b],
             device_id=dev(my_e, far_f), device_id_type=MESH)
 
+    upper = 4 * my_p >= members
+
     def group_of(g):
-        return lax.rem(2 * my_p + g, members)
+        k = jnp.where(g < 2, 1 - g, g)
+        return lax.rem(jnp.where(upper, 2 * my_p + 1 - k, 2 * my_p + k) + members, members)
 
     def i_am_near(fs):
         return near_of(fs, my_p) == my_f
@@ -253,22 +256,31 @@
     def box_of(fs, i):
         return lax.rem(my_e + i, columns) * members + fs
 
-    def pass_on(g):
-        fs = group_of(g)
-
-        def one(i, _):
-            b = box_of(fs, i)
-
-            @pl.when(b != me)
-            def _():
-                forward(b).wait_recv()
-
-            @pl.when(i_am_near(fs))
-            def _():
+    def pass_on(k):
+        fs = jnp.where(lax.rem(my_f, 2) == 1, my_f + k, my_f - k)
+
+        @pl.when(inside(fs, members))
+        def _():
+            def one(i, _):
+                b = box_of(fs, i)
+
+                @pl.when(b != me)
+                def _():
+                    forward(b).wait_recv()
+
                 forward(b).start()
-            return 0
-
-        lax.fori_loop(0, columns, one, 0)
+                return 0
+
+            lax.fori_loop(0, columns, one, 0)
+
+    def passed_here(fs):
+        @pl.when(jnp.logical_not(i_am_near(fs)))
+        def _():
+            def one(i, _):
+                forward(box_of(fs, i)).wait_recv()
+                return 0
+
+            lax.fori_loop(0, columns, one, 0)
 
     def give(b):
         return pltpu.make_async_remote_copy(
@@ -286,6 +298,7 @@
 
     def expert(g):
         fs = group_of(g)
+        passed_here(fs)
         x = jnp.concatenate([inbox[e * members + fs] for e in range(columns)], axis=0)
         gate = lax.dot_general(x, gu[0], nt, preferred_element_type=jnp.float32)
         up = lax.dot_general(x, gu[1], nt, preferred_element_type=jnp.float32)

time: 203 us -> 162 us (0.80)
  the two profiles are of different devices: /device:TPU:25 before, /device:TPU:0 now
where the time goes in v2:
time: 162 us
  Pallas kernels  157 us (97%)
  local copies, waits for them, and re-layouts  5.05 us (3%)
    pallas_call x1, Pallas kernels, on_device(): call(tokens, context, out_proj, norm_gain.reshape(1, width), router, expe...  157 us
    unnamed x3, local copies, waits for them, and re-layouts  5.05 us

profile of v2, /device:TPU:0, one launch (start us, length us, event | category | flops | bytes accessed | tf_op | source)
XLA Modules:
  0.0 162.0 jit_solution(6863482289702129865)
XLA Ops:
  0.0 1.4 copy.10.ids
  1.4 1.8 %copy.9.router = bf16[2048,8]{1,0:T(8,128)(2,1)} copy(bf16[2048,8]{0,1:T(8,128)(2,1)} %param.12) | data formatting | bytes 65536 | tf_op args[4]
  3.2 156.9 %shard_map.82 = bf16[128,2048]{1,0:T(8,128)(2,1)} custom-call(bf16[128,2048]{1,0:T(8,128)(2,1)} %tok.1, bf16[128,2048]{1,0:T(8,128)(2,1)} %ctx.1, bf16[128,2048]{1,0:T(8,128)(2,1)} %wout.1, f32[1,2048]{1,0:T(1,128)} %bitcast.1, bf16[2048,8]{1,0:T(8,128)(2,1)} %copy.9.router, s32[128,2]{1,0:T(8,128)} %copy.10.ids, bf16[1,2,704,2048]{3,2,1,0:T(8,128)(2,1)} %gu_hbm.1, ...), custom_call_target="tpu_custom_call" | custom-call | tf_op jit(solution)/shard_map/pallas_call | solution.py:443
  160.1 1.9 %copy.12 = bf16[128,2048]{1,0:T(8,128)(2,1)} copy(bf16[128,2048]{1,0:T(8,128)(2,1)} %shard_map.82) | data formatting | bytes 1048576

commit v3 on v2

--- a/solution.py
+++ b/solution.py
@@ -165,7 +165,11 @@
             for s in range(members):
                 y_step(t, s)
 
-    id0, id1 = ids[:, 0:1], ids[:, 1:2]
+    diagonal = jnp.where(
+        lax.broadcasted_iota(jnp.int32, (rows, rows), 0) == lax.broadcasted_iota(jnp.int32, (rows, rows), 1), 1.0, 0.0)
+    named_ids = ids[...].astype(jnp.float32)
+    id0 = jnp.sum(diagonal * named_ids[0:1], axis=1, keepdims=True).astype(jnp.int32)
+    id1 = jnp.sum(diagonal * named_ids[1:2], axis=1, keepdims=True).astype(jnp.int32)
     named = lax.broadcasted_iota(jnp.int32, (rows, experts), 1)
     hot0 = jnp.where(named == id0, 1.0, 0.0)
     hot1 = jnp.where(named == id1, 1.0, 0.0)
@@ -336,7 +340,7 @@
 
             lax.fori_loop(0, columns, one, 0)
 
-    logits = jnp.dot(normed, router[...], preferred_element_type=jnp.float32)
+    logits = lax.dot_general(normed, router[...], nt, preferred_element_type=jnp.float32)
     s0 = jax.nn.sigmoid(jnp.sum(logits * hot0, axis=1, keepdims=True))
     s1 = jax.nn.sigmoid(jnp.sum(logits * hot1, axis=1, keepdims=True))
     total = s0 + s1
@@ -440,7 +444,7 @@
         compiler_params=pltpu.CompilerParams(
             collective_id=0, has_side_effects=True, vmem_limit_bytes=VMEM_GRANT),
     )
-    return call(tokens, context, out_proj, norm_gain.reshape(1, width), router, expert_ids, w_gate_up, w_down)
+    return call(tokens, context, out_proj, norm_gain.reshape(1, width), router.T, expert_ids.T, w_gate_up, w_down)
 
 
 def solution(mesh):

time: 162 us -> 159 us (0.981)
  local copies, waits for them, and re-layouts: 5.05 us -> 1.88 us
    unnamed x3 -> x1, local copies, waits for them, and re-layouts: 5.05 us -> 1.88 us
where the time goes in v3:
time: 159 us; the launch traced here: 158 us
  Pallas kernels  156 us (98%)
  local copies, waits for them, and re-layouts  1.88 us (1%)
    pallas_call x1, Pallas kernels, on_device(): call(tokens, context, out_proj, norm_gain.reshape(1, width), router.T, ex...  156 us

profile of v3, /device:TPU:0, one launch (start us, length us, event | category | flops | bytes accessed | tf_op | source)
XLA Modules:
  0.0 158.3 jit_solution(7698434091408725219)
XLA Ops:
  0.0 156.4 %shard_map.82 = bf16[128,2048]{1,0:T(8,128)(2,1)} custom-call(bf16[128,2048]{1,0:T(8,128)(2,1)} %tok.1, bf16[128,2048]{1,0:T(8,128)(2,1)} %ctx.1, bf16[128,2048]{1,0:T(8,128)(2,1)} %wout.1, f32[1,2048]{1,0:T(1,128)} %bitcast.4, bf16[8,2048]{1,0:T(8,128)(2,1)} %bitcast.3, s32[2,128]{1,0:T(2,128)} %bitcast.5, bf16[1,2,704,2048]{3,2,1,0:T(8,128)(2,1)} %gu_hbm.1, ...), custom_call_target="tpu_custom_call" | custom-call | tf_op jit(solution)/shard_map/pallas_call | solution.py:447
  156.4 1.9 %copy.10 = bf16[128,2048]{1,0:T(8,128)(2,1)} copy(bf16[128,2048]{1,0:T(8,128)(2,1)} %shard_map.82) | data formatting | bytes 1048576
